TPU v7x, 32 devices: a whole 2x2x4 slice. The times are simulated.
32 devices in a mesh: dp: 8 (over z, y), neg: 4 (over x, core).
Axes of the slice: x: 2, y: 2, z: 4, core: 2. Of those that a mesh axis runs over, the one named last changes fastest.
Arguments:
- query_features: bfloat16 [8192, 512], P(('dp', 'neg')), may hold values from -8 to 8
- positive_features: bfloat16 [8192, 512], P(('dp', 'neg')), may hold values from -6 to 6
- negative_features: bfloat16 [16384, 512], P(('neg', 'dp')), may hold values from -6 to 6
- positive_ids: int32 [8192], P('dp'), may hold values from 0 to 8191, as said below
- positive_counts: int32 [8192], P(('dp', 'neg')), may hold values from 1 to 16
- negative_ids: int32 [16384], P('neg'), may hold values from 0 to 4095, as said below
- negative_counts: int32 [16384], P('neg'), may hold values from 64 to 4096
- query_first: bfloat16 [512, 1024], replicated, may hold values from -0.25 to 0.25
- query_second: bfloat16 [1024, 512], replicated, may hold values from -0.1875 to 0.1875
- query_third: bfloat16 [512, 256], replicated, may hold values from -0.25 to 0.25
- item_first: bfloat16 [512, 1024], replicated, may hold values from -0.25 to 0.25
- item_second: bfloat16 [1024, 512], replicated, may hold values from -0.1875 to 0.1875
- item_third: bfloat16 [512, 256], replicated, may hold values from -0.25 to 0.25
Outputs:
- mean_loss: float32 [], replicated
- clipped_query_first: float32 [512, 1024], P('dp')
- clipped_query_second: float32 [1024, 512], P('dp')
- clipped_query_third: float32 [512, 256], P('dp')
- clipped_item_first: float32 [512, 1024], P('dp')
- clipped_item_second: float32 [1024, 512], P('dp')
- clipped_item_third: float32 [512, 256], P('dp')
Inputs may be any that keep to these rules, and one draw needn't show every extreme that they name: `negative_ids`: ids of the sampled negatives; one id may stand for several negatives. `positive_ids`: A query's positive id may equal the ids of some negatives; those negatives are left out of that query's denominator.
All inputs are finite; a program needn't handle non-finite values.
Results may differ from a plain program's by a relative error of at most 0.0075.
Values may be sent and summed in bfloat16 or wider, within the bound.
A program may use at most 128 MiB of HBM per device.

v0:
```python
import jax
import jax.numpy as jnp
from jax import lax
from jax.sharding import PartitionSpec as P

inv_temp = 20.0
clip_norm = 256.0


def silu_slope(pre):
    sigma = jax.nn.sigmoid(pre)
    return sigma * (1.0 + pre * (1.0 - sigma))


def contract_rows(left, right):
    return lax.dot_general(
        left, right, (((0,), (0,)), ((), ())), preferred_element_type=jnp.float32
    )


def contract_cols(left, right):
    return lax.dot_general(
        left, right, (((1,), (1,)), ((), ())), preferred_element_type=jnp.float32
    )


def tower_forward(features, first, second, third):
    first_pre = jnp.dot(features, first, preferred_element_type=jnp.float32)
    first_act = jax.nn.silu(first_pre).astype(jnp.bfloat16)
    second_pre = jnp.dot(first_act, second, preferred_element_type=jnp.float32)
    second_act = jax.nn.silu(second_pre).astype(jnp.bfloat16)
    embedding = jnp.dot(second_act, third, preferred_element_type=jnp.float32)
    inv_norm = lax.rsqrt(jnp.sum(embedding * embedding, axis=1, keepdims=True) + 1.0)
    unit = (embedding * inv_norm).astype(jnp.bfloat16)
    return ((first_pre, first_act, second_pre, second_act, embedding, inv_norm), unit)


def tower_backward(features, second, third, saved, unit_grad):
    first_pre, first_act, second_pre, second_act, embedding, inv_norm = saved
    along = jnp.sum(embedding * unit_grad, axis=1, keepdims=True)
    embed_grad = (inv_norm * unit_grad - inv_norm * inv_norm * inv_norm * embedding * along).astype(
        jnp.bfloat16
    )
    third_grad = contract_rows(second_act, embed_grad)
    second_slope = (contract_cols(embed_grad, third) * silu_slope(second_pre)).astype(jnp.bfloat16)
    second_grad = contract_rows(first_act, second_slope)
    first_slope = (contract_cols(second_slope, second) * silu_slope(first_pre)).astype(jnp.bfloat16)
    first_grad = contract_rows(features, first_slope)
    return (first_grad, second_grad, third_grad)


def per_device(
    query_features,
    positive_features,
    negative_features,
    positive_ids,
    positive_counts,
    negative_ids,
    negative_counts,
    query_first,
    query_second,
    query_third,
    item_first,
    item_second,
    item_third,
):
    own_rows = query_features.shape[0]
    query_saved, query_unit = tower_forward(query_features, query_first, query_second, query_third)
    item_features = jnp.concatenate([positive_features, negative_features], axis=0)
    item_saved, item_unit = tower_forward(item_features, item_first, item_second, item_third)
    positive_unit = item_unit[:own_rows]
    negative_unit = item_unit[own_rows:]
    group_unit = lax.all_gather(query_unit, "neg", axis=0, tiled=True)
    shard_unit = lax.all_gather(negative_unit, "dp", axis=0, tiled=True)
    scores = (
        contract_cols(group_unit, shard_unit) * inv_temp
        - jnp.log(negative_counts.astype(jnp.float32))[None, :]
    )
    weights = jnp.where(positive_ids[:, None] != negative_ids[None, :], jnp.exp(scores), 0.0)
    positive_logit = jnp.sum(
        query_unit.astype(jnp.float32) * positive_unit.astype(jnp.float32), axis=1
    ) * inv_temp - jnp.log(positive_counts.astype(jnp.float32))
    positive_exp = jnp.exp(positive_logit)
    offset = lax.axis_index("neg") * own_rows
    partial_value = jnp.sum(weights, axis=1)
    own_part = lax.dynamic_slice(partial_value, (offset,), (own_rows,)) + positive_exp
    partial_value = lax.dynamic_update_slice(partial_value, own_part, (offset,))
    denom = lax.psum(partial_value, "neg")
    own_denom = lax.dynamic_slice(denom, (offset,), (own_rows,))
    loss_part = jnp.sum(jnp.log(own_denom) - positive_logit)
    softmax_weights = (weights / denom[:, None]).astype(jnp.bfloat16)
    positive_slope = positive_exp / own_denom - 1.0
    block = softmax_weights
    query_sum = lax.psum_scatter(
        jnp.dot(block, shard_unit, preferred_element_type=jnp.float32),
        "neg",
        scatter_dimension=0,
        tiled=True,
    )
    query_grad = (
        query_sum + positive_slope[:, None] * positive_unit.astype(jnp.float32)
    ) * inv_temp
    block = softmax_weights
    negative_sum = lax.psum_scatter(
        contract_rows(block, group_unit), "dp", scatter_dimension=0, tiled=True
    )
    positive_grad = positive_slope[:, None] * query_unit.astype(jnp.float32) * inv_temp
    item_grad = jnp.concatenate([positive_grad, negative_sum * inv_temp], axis=0)
    query_grads = tower_backward(query_features, query_second, query_third, query_saved, query_grad)
    item_grads = tower_backward(item_features, item_second, item_third, item_saved, item_grad)
    gradients = query_grads + item_grads
    loss_sum = lax.psum(loss_part, ("dp", "neg"))
    mean_loss = loss_sum / (own_rows * lax.axis_size("dp") * lax.axis_size("neg"))
    vectors = tuple((gradient.reshape(-1) for gradient in gradients))
    pieces = (
        lax.psum_scatter(vectors[0], ("dp", "neg"), scatter_dimension=0, tiled=True),
        lax.psum_scatter(vectors[1], ("dp", "neg"), scatter_dimension=0, tiled=True),
        lax.psum_scatter(vectors[2], ("dp", "neg"), scatter_dimension=0, tiled=True),
        lax.psum_scatter(vectors[3], ("dp", "neg"), scatter_dimension=0, tiled=True),
        lax.psum_scatter(vectors[4], ("dp", "neg"), scatter_dimension=0, tiled=True),
        lax.psum_scatter(vectors[5], ("dp", "neg"), scatter_dimension=0, tiled=True),
    )
    squares = jnp.zeros((), jnp.float32)
    for piece in pieces:
        squares = squares + jnp.sum(piece * piece)
    grad_norm = jnp.sqrt(lax.psum(squares, ("dp", "neg")))
    clip_factor = clip_norm / jnp.maximum(grad_norm, clip_norm)
    scaled = tuple((piece * clip_factor for piece in pieces))
    gathered = (
        lax.all_gather(scaled[0], "neg", axis=0, tiled=True),
        lax.all_gather(scaled[1], "neg", axis=0, tiled=True),
        lax.all_gather(scaled[2], "neg", axis=0, tiled=True),
        lax.all_gather(scaled[3], "neg", axis=0, tiled=True),
        lax.all_gather(scaled[4], "neg", axis=0, tiled=True),
        lax.all_gather(scaled[5], "neg", axis=0, tiled=True),
    )
    clipped = tuple(
        (vector.reshape(-1, gradient.shape[1]) for vector, gradient in zip(gathered, gradients))
    )
    return (mean_loss, clipped[0], clipped[1], clipped[2], clipped[3], clipped[4], clipped[5])


def solution(mesh):
    placed = (
        P(("dp", "neg"), None),
        P(("dp", "neg"), None),
        P(("neg", "dp"), None),
        P("dp"),
        P(("dp", "neg")),
        P("neg"),
        P("neg"),
        P(),
        P(),
        P(),
        P(),
        P(),
        P(),
    )
    return jax.shard_map(
        per_device,
        mesh=mesh,
        in_specs=placed,
        out_specs=(
            P(),
            P("dp", None),
            P("dp", None),
            P("dp", None),
            P("dp", None),
            P("dp", None),
            P("dp", None),
        ),
        check_vma=False,
    )
```

profile of v0, /device:TPU:0, one launch (start us, length us, event | category | flops | bytes accessed | tf_op | source)
XLA Modules:
  0.0 522.5 jit_solution(4157057472190406445)
XLA Ops:
  9.4 2.9 multiply_convert_fusion.1
  12.3 2.3 multiply_convert_fusion.3
  17.3 2.9 multiply_convert_fusion.6
  21.0 8.6 %all_gather.24 = bf16[1024,256]{0,1:T(8,128)(2,1)S(1)} all-gather(bf16[256,256]{0,1:T(8,128)(2,1)S(1)} %get-tuple-element.16), channel_id=1, replica_groups=mesh['dp'=8,'neg'=4] {'neg'}, dimensions={0}, use_global_device_ids=true | all-gather | bytes 655360 | tf_op jit(solution)/shard_map/all_gather | solution.py:73
  29.6 40.3 %all-gather.2.cloned.1.call-done = bf16[4096,256]{0,1:T(8,128)(2,1)} async-done(((bf16[512,256]{0,1:T(8,128)(2,1)}), bf16[4096,256]{0,1:T(8,128)(2,1)}) %all-gather.2.cloned.1.call-update) | async-done | bytes 2097168 | tf_op jit(solution)/shard_map/all_gather | solution.py:74
  70.0 9.7 %fusion = (f32[1024]{0:T(1024)S(1)}, f32[1024,4096]{1,0:T(8,128)}) fusion(f32[4096]{0:T(1024)S(1)} %convert_log_fusion, s32[4096]{0:T(1024)S(1)} %copy-done.18, s32[1024]{0:T(1024)S(1)} %copy-done.19, bf16[1024,256]{0,1:T(8,128)(2,1)S(1)} %all_gather.24, bf16[4096,256]{0,1:T(8,128)(2,1)} %all-gather.2.cloned.1.call-done), kind=kOutput, calls=%fused_computation.2 | convolution fusion | flops 2168454144 | bytes 19439616 | tf_op jit(solution)/shard_map/dot_general | solution.py:22
  79.8 5.8 %psum.21 = f32[1024]{0:T(1024)S(1)} all-reduce(f32[1024]{0:T(1024)S(1)} %add_dynamic-update-slice_fusion), channel_id=1, replica_groups=mesh['dp'=8,'neg'=4] {'neg'}, use_global_device_ids=true, to_apply=%region_4.5 | all-reduce | flops 1024 | bytes 8192 | tf_op jit(solution)/shard_map/psum | solution.py:88
  85.6 8.4 %divide_convert_fusion = bf16[1024,4096]{1,0:T(8,128)(2,1)S(1)} fusion(f32[1024,4096]{1,0:T(8,128)} %get-tuple-element.37, f32[1024]{0:T(1024)S(1)} %psum.21, f32[4096]{0:T(1024)S(1)} %convert_log_fusion, s32[4096]{0:T(1024)S(1)} %copy-done.18, s32[1024]{0:T(1024)S(1)} %copy-done.19), kind=kLoop, calls=%fused_computation | loop fusion | flops 25165824 | bytes 25206784 | tf_op jit(solution)/shard_map/convert_element_type | solution.py:91
  94.0 3.2 copy-done.2
  97.2 3.3 fusion.15
  100.8 7.7 %fusion.16 = f32[4096,256]{0,1:T(8,128)} fusion(bf16[1024,256]{0,1:T(8,128)(2,1)S(1)} %all_gather.24, bf16[1024,4096]{1,0:T(8,128)(2,1)} %copy-done.2), kind=kOutput, calls=%fused_computation.73 | convolution fusion | flops 2147483648 | bytes 13107200 | tf_op jit(solution)/shard_map/dot_general | solution.py:16
  109.2 14.5 %reduce-scatter.3.cloned.1.call-done = f32[256,256]{0,1:T(8,128)} async-done(((f32[1024,256]{0,1:T(8,128)}), f32[256,256]{0,1:T(8,128)}) %reduce-scatter.3.cloned.1.call-update) | async-done | bytes 262160 | tf_op jit(solution)/shard_map/reduce_scatter | solution.py:94
  125.9 1.4 fusion.2
  127.3 3.5 convolution_bitcast_fusion.1
  130.8 1.9 copy.26
  132.7 1.8 copy.30
  135.1 1.9 copy.31
  138.3 77.8 %reduce-scatter.5.cloned.1.call-done = f32[512,256]{0,1:T(8,128)} async-done(((f32[4096,256]{0,1:T(8,128)}), f32[512,256]{0,1:T(8,128)}) %reduce-scatter.5.cloned.1.call-update) | async-done | bytes 524304 | tf_op jit(solution)/shard_map/reduce_scatter | solution.py:104
  221.7 1.9 copy.34
  223.6 4.5 convolution_bitcast_fusion.3
  228.1 1.8 copy.33
  229.9 191.2 %all-reduce.10.cloned.1.call-done = (f32[524288]{0:T(1024)}, f32[524288]{0:T(1024)}, f32[131072]{0:T(1024)}, f32[524288]{0:T(1024)}, f32[524288]{0:T(1024)}, /*index=5*/f32[131072]{0:T(1024)}) async-done(((f32[524288]{0:T(1024)}, f32[524288]{0:T(1024)}, f32[131072]{0:T(1024)}, f32[524288]{0:T(1024)}, f32[524288]{0:T(1024)}, /*index=5*/f32[131072]{0:T(1024)}), (f32[524288]{0:T(1024)}, f32[524288]{0:T(1024)}, ...) | async-done | bytes 9437200
  421.1 1.5 multiply_reduce_fusion.4
  422.6 1.5 multiply_reduce_fusion.6
  425.4 1.4 multiply_reduce_fusion.8
  429.4 40.4 %all-reduce.6 = (f32[]{:T(128)}, f32[]{:T(128)}) all-reduce(f32[]{:T(128)} %get-tuple-element.18, f32[]{:T(128)S(6)} %add.128), channel_id=1, replica_groups=mesh['dp'=8,'neg'=4] {'dp','neg'}, use_global_device_ids=true, to_apply=%region_6.7 | all-reduce | flops 2 | bytes 16 | tf_op jit(solution)/shard_map/psum | solution.py:112
  475.5 5.5 %all_gather.31 = f32[16384]{0:T(1024)S(1)} all-gather(f32[4096]{0:T(1024)S(1)} %dynamic-slice_multiply_fusion.4), channel_id=1, replica_groups=mesh['dp'=8,'neg'=4] {'neg'}, dimensions={0}, use_global_device_ids=true | all-gather | bytes 81920 | tf_op jit(solution)/shard_map/all_gather | solution.py:135
  481.6 6.3 %all_gather.30 = f32[65536]{0:T(1024)S(1)} all-gather(f32[16384]{0:T(1024)S(1)} %dynamic-slice_multiply_fusion), channel_id=1, replica_groups=mesh['dp'=8,'neg'=4] {'neg'}, dimensions={0}, use_global_device_ids=true | all-gather | bytes 327680 | tf_op jit(solution)/shard_map/all_gather | solution.py:134
  488.6 5.8 %all_gather.29 = f32[65536]{0:T(1024)S(1)} all-gather(f32[16384]{0:T(1024)S(1)} %dynamic-slice_multiply_fusion.1), channel_id=1, replica_groups=mesh['dp'=8,'neg'=4] {'neg'}, dimensions={0}, use_global_device_ids=true | all-gather | bytes 327680 | tf_op jit(solution)/shard_map/all_gather | solution.py:133
  495.2 5.2 all_gather.28
  501.0 5.8 %all_gather.27 = f32[65536]{0:T(1024)S(1)} all-gather(f32[16384]{0:T(1024)S(1)} %dynamic-slice_multiply_fusion.2), channel_id=1, replica_groups=mesh['dp'=8,'neg'=4] {'neg'}, dimensions={0}, use_global_device_ids=true | all-gather | bytes 327680 | tf_op jit(solution)/shard_map/all_gather | solution.py:131
  507.6 5.8 %all_gather.26 = f32[65536]{0:T(1024)S(1)} all-gather(f32[16384]{0:T(1024)S(1)} %dynamic-slice_multiply_fusion.3), channel_id=1, replica_groups=mesh['dp'=8,'neg'=4] {'neg'}, dimensions={0}, use_global_device_ids=true | all-gather | bytes 327680 | tf_op jit(solution)/shard_map/all_gather | solution.py:130
  (98 shorter events, 25.5 us)
Async XLA Ops:
  7.2 2.2 copy-start
  7.2 62.8 %all-gather.2.cloned.1.call-start = ((), (), s32[]{:S(2)}) async-start(), calls=%async_computation.2 | async-start | bytes 2359296 | tf_op jit(solution)/shard_map/all_gather | solution.py:74
  9.4 2.9 copy-start.15
  9.4 2.9 copy-start.22
  12.3 2.3 copy-start.23
  12.3 3.2 copy-start.12
  14.6 0.9 copy-start.3
  14.6 2.2 copy-start.7
  14.6 2.2 copy-start.11
  16.7 107.0 %reduce-scatter.3.cloned.1.call-start = ((), (), s32[]{:S(2)}) async-start(), calls=%async_computation.3 | async-start | bytes 1310720 | tf_op jit(solution)/shard_map/reduce_scatter | solution.py:94
  17.2 3.0 copy-start.8
  17.2 3.0 copy-start.14
  17.3 12.3 %copy-start.17 = (s32[4096]{0:T(1024)S(1)}, s32[4096]{0:T(1024)}, u32[]{:S(2)}) copy-start(s32[4096]{0:T(1024)} %param.19) | copy-start | bytes 49156
  17.3 52.7 %copy-start.18 = (s32[4096]{0:T(1024)S(1)}, s32[4096]{0:T(1024)}, u32[]{:S(2)}) copy-start(s32[4096]{0:T(1024)} %param.18) | copy-start | bytes 49156
  17.3 52.7 %copy-start.19 = (s32[1024]{0:T(1024)S(1)}, s32[1024]{0:T(1024)}, u32[]{:S(2)}) copy-start(s32[1024]{0:T(1024)} %param.16) | copy-start | bytes 12292
  20.2 0.7 copy-start.5
  29.6 50.0 %copy-start.20 = (s32[256]{0:T(256)S(1)}, s32[256]{0:T(256)}, u32[]{:S(2)}) copy-start(s32[256]{0:T(256)} %param.17) | copy-start | bytes 3076
  85.6 11.6 %copy-start.21 = (bf16[4096,256]{0,1:T(8,128)(2,1)S(1)}, bf16[4096,256]{0,1:T(8,128)(2,1)}, u32[]{:S(2)}) copy-start(bf16[4096,256]{0,1:T(8,128)(2,1)} %all-gather.2.cloned.1.call-done) | copy-start | bytes 6291460
  94.0 3.2 copy-start.2
  100.6 115.6 %reduce-scatter.5.cloned.1.call-start = ((), (), s32[]{:S(2)}) async-start(), calls=%async_computation.4 | async-start | bytes 4718592 | tf_op jit(solution)/shard_map/reduce_scatter | solution.py:104
  108.5 312.6 %all-reduce.10.cloned.1.call-start = ((), (), s32[]{:S(2)}) async-start(), calls=%async_computation.5 | async-start | bytes 18874368
  124.8 2.5 copy-start.9
  132.7 1.8 copy-start.10
  135.0 1.9 copy-start.6
  138.3 79.2 %copy-start.4 = (bf16[768,512]{1,0:T(8,128)(2,1)S(1)}, bf16[768,512]{1,0:T(8,128)(2,1)}, u32[]{:S(2)}) copy-start(bf16[768,512]{1,0:T(8,128)(2,1)} %copy-done.3) | copy-start | bytes 2359300
  217.3 1.7 copy-start.13
  217.3 1.7 copy-start.26
  219.1 1.6 copy-start.24
  219.8 0.9 copy-start.25
  221.7 1.9 copy-start.16
  472.1 42.7 %copy-start.1 = (bf16[512,1024]{1,0:T(8,128)(2,1)S(1)}, bf16[512,1024]{1,0:T(8,128)(2,1)}, u32[]{:S(2)}) copy-start(bf16[512,1024]{1,0:T(8,128)(2,1)} %param.23) | copy-start | bytes 3145732
Sparse Core Ops, SparseCore 0:
  16.8 53.0 all-gather.1
  100.7 23.0 reduce-scatter.2
  127.4 88.6 reduce-scatter.4
  230.0 191.0 all-reduce.9
where the time goes:
time: 524 us; the launch traced here: 523 us
  waiting for transfers between devices  324 us (62%)
  blocking collectives  89.4 us (17%)
  matrix products  42.1 us (8%)
  local copies, waits for them, and re-layouts  24.1 us (5%)
  other arithmetic  22.1 us (4%)
  between operations  20.5 us (4%)
    unnamed x5, waiting for transfers between devices  191 us
    reduce_scatter x1, waiting for transfers between devices, per_device(): lax.psum_scatter(contract_rows(block, group_unit), 'dp', scatter_dimensio...  77.8 us
    psum x1, blocking collectives, per_device(): loss_sum = lax.psum(loss_part, ('dp', 'neg'))  40.4 us
    all_gather x1, waiting for transfers between devices, per_device(): shard_unit = lax.all_gather(negative_unit, 'dp', axis=0, tiled=True)  40.3 us
    dot_general x7, matrix products, contract_rows(): lax.dot_general(left, right, (((0,), (0,)), ((), ())), preferred_element_...  17.9 us
    unnamed x61, local copies, waits for them, and re-layouts  16.1 us
    reduce_scatter x1, waiting for transfers between devices, per_device(): lax.psum_scatter(jnp.dot(block, shard_unit, preferred_element_type=jnp.fl...  14.5 us
    dot_general x3, matrix products, contract_cols(): lax.dot_general(left, right, (((1,), (1,)), ((), ())), preferred_element_...  11.7 us
  transfers between devices with their start and end apart: 4, of which 4 were waited for; matrix products, arithmetic and copies ran while one was open for 5% of the time, Pallas kernels for 0%

commit v1 on v0

--- a/solution.py
+++ b/solution.py
@@ -71,7 +71,14 @@
     positive_unit = item_unit[:own_rows]
     negative_unit = item_unit[own_rows:]
     group_unit = lax.all_gather(query_unit, "neg", axis=0, tiled=True)
-    shard_unit = lax.all_gather(negative_unit, "dp", axis=0, tiled=True)
+    ways, here, step = (lax.axis_size("dp"), lax.axis_index("dp"), negative_unit.shape[0])
+    line, have = (negative_unit, 1)
+    while have < ways:
+        line = jnp.concatenate(
+            [line, lax.ppermute(line, "dp", [(d, (d - have) % ways) for d in range(ways)])], axis=0
+        )
+        have = 2 * have
+    shard_unit = jnp.roll(line, here * step, axis=0)
     scores = (
         contract_cols(group_unit, shard_unit) * inv_temp
         - jnp.log(negative_counts.astype(jnp.float32))[None, :]

time: 524 us -> 543 us (1.036)
  waiting for transfers between devices: 324 us -> 339 us
  starting transfers between devices: 0.34 us -> 8.49 us
    ppermute x0 -> x3, waiting for transfers between devices: none -> 52.2 us  [per_device(): lax.ppermute(line, 'dp', [(d, (d - have) % ways) for d in range(ways)])]
    all_gather x1 -> x0, waiting for transfers between devices: 40.3 us -> none  [per_device(): shard_unit = lax.all_gather(negative_unit, 'dp', axis=0, tiled=True)]
    ppermute x0 -> x3, starting transfers between devices: none -> 8.19 us  [per_device(): lax.ppermute(line, 'dp', [(d, (d - have) % ways) for d in range(ways)])]
    unnamed x61 -> x75, local copies, waits for them, and re-layouts: 16.1 us -> 15.7 us
    unnamed x5 -> x4, waiting for transfers between devices: 191 us -> 191 us
  transfers between devices with their start and end apart: 4 -> 6, of which waited for: 4 -> 6; matrix products, arithmetic and copies ran while one was open for 5% -> 5% of each run, Pallas kernels for 0% -> 0%
where the time goes in v1:
time: 543 us; the launch traced here: 542 us
  waiting for transfers between devices  339 us (62%)
  blocking collectives  88.1 us (16%)
  matrix products  39.2 us (7%)
  local copies, waits for them, and re-layouts  23.9 us (4%)
  other arithmetic  22.8 us (4%)
  between operations  20.6 us (4%)
  starting transfers between devices  8.49 us (2%)
    unnamed x4, waiting for transfers between devices  191 us
    reduce_scatter x1, waiting for transfers between devices, per_device(): lax.psum_scatter(contract_rows(block, group_unit), 'dp', scatter_dimensio...  77.8 us
    ppermute x3, waiting for transfers between devices, per_device(): lax.ppermute(line, 'dp', [(d, (d - have) % ways) for d in range(ways)])  52.2 us
    psum x1, blocking collectives, per_device(): loss_sum = lax.psum(loss_part, ('dp', 'neg'))  40.5 us
    reduce_scatter x1, waiting for transfers between devices, per_device(): lax.psum_scatter(jnp.dot(block, shard_unit, preferred_element_type=jnp.fl...  18 us
    dot_general x7, matrix products, contract_rows(): lax.dot_general(left, right, (((0,), (0,)), ((), ())), preferred_element_...  17.9 us
    unnamed x75, local copies, waits for them, and re-layouts  15.7 us
  transfers between devices with their start and end apart: 6, of which 6 were waited for; matrix products, arithmetic and copies ran while one was open for 5% of the time, Pallas kernels for 0%

profile of v1, /device:TPU:0, one launch (start us, length us, event | category | flops | bytes accessed | tf_op | source)
XLA Modules:
  0.0 542.3 jit_solution(18061602306348163416)
XLA Ops:
  9.4 2.9 multiply_convert_fusion.1
  12.3 2.3 multiply_convert_fusion.3
  15.9 6.0 %collective-permute-start = (bf16[512,256]{0,1:T(8,128)(2,1)S(1)}, bf16[512,256]{0,1:T(8,128)(2,1)S(1)}, u32[]{:S(2)}, u32[]{:S(2)}) collective-permute-start(bf16[512,256]{0,1:T(8,128)(2,1)S(1)} %get-tuple-element.17), channel_id=1, source_target_pairs={{0,28},{4,0},{8,4},{12,8},{16,12},{20,16},{24,20},{28,24},{1,29},{... | collective-permute-start | bytes 786440 | tf_op jit(solution)/shard_map/ppermute | solution.py:78
  22.4 5.1 collective-permute-done
  27.6 1.6 collective-permute-start.1
  31.4 9.0 %collective-permute-done.1 = bf16[1024,256]{0,1:T(8,128)(2,1)S(1)} collective-permute-done((bf16[1024,256]{0,1:T(8,128)(2,1)S(1)}, bf16[1024,256]{0,1:T(8,128)(2,1)S(1)}, u32[]{:S(2)}, u32[]{:S(2)}) %collective-permute-start.1) | collective-permute-done | bytes 524320 | tf_op jit(solution)/shard_map/ppermute | solution.py:78
  41.8 7.2 %all_gather.21 = bf16[1024,256]{0,1:T(8,128)(2,1)S(1)} all-gather(bf16[256,256]{0,1:T(8,128)(2,1)S(1)} %get-tuple-element.16), channel_id=1, replica_groups=mesh['dp'=8,'neg'=4] {'neg'}, dimensions={0}, use_global_device_ids=true | all-gather | bytes 655360 | tf_op jit(solution)/shard_map/all_gather | solution.py:73
  49.0 38.1 %collective-permute-done.2 = bf16[2048,256]{0,1:T(8,128)(2,1)S(1)} collective-permute-done((bf16[2048,256]{0,1:T(8,128)(2,1)S(1)}, bf16[2048,256]{0,1:T(8,128)(2,1)S(1)}, u32[]{:S(2)}, u32[]{:S(2)}) %collective-permute-start.2) | collective-permute-done | bytes 1048608 | tf_op jit(solution)/shard_map/ppermute | solution.py:78
  87.5 8.2 %fusion = (f32[1024]{0:T(1024)S(1)}, f32[1024,4096]{1,0:T(8,128)}) fusion(f32[4096]{0:T(1024)S(1)} %convert_log_fusion, s32[4096]{0:T(1024)S(1)} %copy-done.22, s32[1024]{0:T(1024)S(1)} %copy-done.23, bf16[1024,256]{0,1:T(8,128)(2,1)S(1)} %all_gather.21, bf16[8192,256]{0,1:T(8,128)(2,1)S(1)} %constant_dynamic-update-slice_fusion.2, s32[]{:T(128)S(6)} %select_n.23), kind=kOutput, calls=%fused_computation.2 | convolution fusion | flops 2168454144 | bytes 19439620 | tf_op jit(solution)/shard_map/dot_general | solution.py:22
  95.8 6.0 %psum.21 = f32[1024]{0:T(1024)S(1)} all-reduce(f32[1024]{0:T(1024)S(1)} %add_dynamic-update-slice_fusion), channel_id=1, replica_groups=mesh['dp'=8,'neg'=4] {'neg'}, use_global_device_ids=true, to_apply=%region_4.5 | all-reduce | flops 1024 | bytes 8192 | tf_op jit(solution)/shard_map/psum | solution.py:95
  101.9 8.5 %divide_convert_fusion = bf16[1024,4096]{1,0:T(8,128)(2,1)S(1)} fusion(f32[1024,4096]{1,0:T(8,128)} %get-tuple-element.39, f32[1024]{0:T(1024)S(1)} %psum.21, f32[4096]{0:T(1024)S(1)} %convert_log_fusion, s32[4096]{0:T(1024)S(1)} %copy-done.22, s32[1024]{0:T(1024)S(1)} %copy-done.23), kind=kLoop, calls=%fused_computation | loop fusion | flops 25165824 | bytes 25206784 | tf_op jit(solution)/shard_map/convert_element_type | solution.py:98
  110.4 3.2 copy-done.2
  113.6 3.4 fusion.1
  117.3 7.7 %fusion.22 = f32[4096,256]{0,1:T(8,128)} fusion(bf16[1024,256]{0,1:T(8,128)(2,1)S(1)} %all_gather.21, bf16[1024,4096]{1,0:T(8,128)(2,1)} %copy-done.2), kind=kOutput, calls=%fused_computation.89 | convolution fusion | flops 2147483648 | bytes 13107200 | tf_op jit(solution)/shard_map/dot_general | solution.py:16
  125.8 18.0 %reduce-scatter.3.cloned.1.call-done = f32[256,256]{0,1:T(8,128)} async-done(((f32[1024,256]{0,1:T(8,128)}), f32[256,256]{0,1:T(8,128)}) %reduce-scatter.3.cloned.1.call-update) | async-done | bytes 262160 | tf_op jit(solution)/shard_map/reduce_scatter | solution.py:101
  147.2 3.5 convolution_bitcast_fusion.1
  150.7 1.9 copy.26
  152.6 1.8 copy.30
  154.9 1.9 copy.31
  158.2 77.8 %reduce-scatter.5.cloned.1.call-done = f32[512,256]{0,1:T(8,128)} async-done(((f32[4096,256]{0,1:T(8,128)}), f32[512,256]{0,1:T(8,128)}) %reduce-scatter.5.cloned.1.call-update) | async-done | bytes 524304 | tf_op jit(solution)/shard_map/reduce_scatter | solution.py:111
  241.6 1.9 copy.34
  243.4 4.5 convolution_bitcast_fusion.3
  248.0 1.8 copy.33
  249.8 191.2 %all-reduce.10.cloned.1.call-done = (f32[524288]{0:T(1024)}, f32[524288]{0:T(1024)}, f32[131072]{0:T(1024)}, f32[524288]{0:T(1024)}, f32[524288]{0:T(1024)}, /*index=5*/f32[131072]{0:T(1024)}) async-done(((f32[524288]{0:T(1024)}, f32[524288]{0:T(1024)}, f32[131072]{0:T(1024)}, f32[524288]{0:T(1024)}, f32[524288]{0:T(1024)}, /*index=5*/f32[131072]{0:T(1024)}), (f32[524288]{0:T(1024)}, f32[524288]{0:T(1024)}, ...) | async-done | bytes 9437200
  441.0 1.5 multiply_reduce_fusion.4
  449.2 40.5 %all-reduce.6 = (f32[]{:T(128)}, f32[]{:T(128)}) all-reduce(f32[]{:T(128)} %get-tuple-element.20, f32[]{:T(128)S(6)} %add.140), channel_id=1, replica_groups=mesh['dp'=8,'neg'=4] {'dp','neg'}, use_global_device_ids=true, to_apply=%region_6.7 | all-reduce | flops 2 | bytes 16 | tf_op jit(solution)/shard_map/psum | solution.py:119
  495.3 5.5 %all_gather.27 = f32[16384]{0:T(1024)S(1)} all-gather(f32[4096]{0:T(1024)S(1)} %dynamic-slice_multiply_fusion.4), channel_id=1, replica_groups=mesh['dp'=8,'neg'=4] {'neg'}, dimensions={0}, use_global_device_ids=true | all-gather | bytes 81920 | tf_op jit(solution)/shard_map/all_gather | solution.py:142
  501.4 6.3 %all_gather.26 = f32[65536]{0:T(1024)S(1)} all-gather(f32[16384]{0:T(1024)S(1)} %dynamic-slice_multiply_fusion), channel_id=1, replica_groups=mesh['dp'=8,'neg'=4] {'neg'}, dimensions={0}, use_global_device_ids=true | all-gather | bytes 327680 | tf_op jit(solution)/shard_map/all_gather | solution.py:141
  508.4 5.8 %all_gather.25 = f32[65536]{0:T(1024)S(1)} all-gather(f32[16384]{0:T(1024)S(1)} %dynamic-slice_multiply_fusion.1), channel_id=1, replica_groups=mesh['dp'=8,'neg'=4] {'neg'}, dimensions={0}, use_global_device_ids=true | all-gather | bytes 327680 | tf_op jit(solution)/shard_map/all_gather | solution.py:140
  515.0 5.2 all_gather.24
  520.8 5.8 %all_gather.23 = f32[65536]{0:T(1024)S(1)} all-gather(f32[16384]{0:T(1024)S(1)} %dynamic-slice_multiply_fusion.2), channel_id=1, replica_groups=mesh['dp'=8,'neg'=4] {'neg'}, dimensions={0}, use_global_device_ids=true | all-gather | bytes 327680 | tf_op jit(solution)/shard_map/all_gather | solution.py:138
  527.4 5.8 %all_gather.22 = f32[65536]{0:T(1024)S(1)} all-gather(f32[16384]{0:T(1024)S(1)} %dynamic-slice_multiply_fusion.3), channel_id=1, replica_groups=mesh['dp'=8,'neg'=4] {'neg'}, dimensions={0}, use_global_device_ids=true | all-gather | bytes 327680 | tf_op jit(solution)/shard_map/all_gather | solution.py:137
  (118 shorter events, 31.8 us)
Async XLA Ops:
  7.2 2.2 copy-start
  7.2 136.5 %reduce-scatter.3.cloned.1.call-start = ((), (), s32[]{:S(2)}) async-start(), calls=%async_computation.2 | async-start | bytes 1310720 | tf_op jit(solution)/shard_map/reduce_scatter | solution.py:101
  9.4 2.9 copy-start.16
  9.4 2.9 copy-start.26
  12.3 2.3 copy-start.27
  12.3 2.3 copy-start.13
  14.6 7.3 %copy-start.7 = (bf16[512,1024]{1,0:T(8,128)(2,1)S(1)}, bf16[512,1024]{1,0:T(8,128)(2,1)}, u32[]{:S(2)}) copy-start(bf16[512,1024]{1,0:T(8,128)(2,1)} %param.20) | copy-start | bytes 3145732
  14.6 7.3 %copy-start.11 = (bf16[256,512]{1,0:T(8,128)(2,1)S(1)}, bf16[256,512]{1,0:T(8,128)(2,1)}, u32[]{:S(2)}) copy-start(bf16[256,512]{1,0:T(8,128)(2,1)} %param.13) | copy-start | bytes 786436
  15.9 11.6 %collective-permute-start = (bf16[512,256]{0,1:T(8,128)(2,1)S(1)}, bf16[512,256]{0,1:T(8,128)(2,1)S(1)}, u32[]{:S(2)}, u32[]{:S(2)}) collective-permute-start(bf16[512,256]{0,1:T(8,128)(2,1)S(1)} %get-tuple-element.17), channel_id=1, source_target_pairs={{0,28},{4,0},{8,4},{12,8},{16,12},{20,16},{24,20},{28,24},{1,29},{... | collective-permute-start | bytes 786440 | tf_op jit(solution)/shard_map/ppermute | solution.py:78
  21.9 7.2 %copy-start.25 = (bf16[1024,512]{1,0:T(8,128)(2,1)S(1)}, bf16[1024,512]{1,0:T(8,128)(2,1)}, u32[]{:S(2)}) copy-start(bf16[1024,512]{1,0:T(8,128)(2,1)} %param.21) | copy-start | bytes 3145732
  22.4 8.1 %copy-start.8 = (f32[256,1024]{1,0:T(8,128)}, f32[256,1024]{1,0:T(8,128)S(1)}, u32[]{:S(2)}) copy-start(f32[256,1024]{1,0:T(8,128)S(1)} %fusion.21) | copy-start | bytes 3145732
  27.6 3.6 copy-start.15
  27.6 12.9 %collective-permute-start.1 = (bf16[1024,256]{0,1:T(8,128)(2,1)S(1)}, bf16[1024,256]{0,1:T(8,128)(2,1)S(1)}, u32[]{:S(2)}, u32[]{:S(2)}) collective-permute-start(bf16[1024,256]{0,1:T(8,128)(2,1)S(1)} %pad_maximum_fusion.2), channel_id=1, source_target_pairs={{0,24},{4,28},{8,0},{12,4},{16,8},{20,12},{24,16},{28,20},{1,25},{... | collective-permute-start | bytes 1572872 | tf_op jit(solution)/shard_map/ppermute | solution.py:78
  29.2 19.8 %copy-start.18 = (bf16[8192,256]{0,1:T(8,128)(2,1)S(1)}, bf16[8192,256]{0,1:T(8,128)(2,1)}, u32[]{:S(2)}) copy-start(bf16[8192,256]{0,1:T(8,128)(2,1)} %get-tuple-element.18) | copy-start | bytes 12582916
  30.4 18.5 %copy-start.21 = (s32[4096]{0:T(1024)S(1)}, s32[4096]{0:T(1024)}, u32[]{:S(2)}) copy-start(s32[4096]{0:T(1024)} %param.19) | copy-start | bytes 49156
  40.5 46.6 %collective-permute-start.2 = (bf16[2048,256]{0,1:T(8,128)(2,1)S(1)}, bf16[2048,256]{0,1:T(8,128)(2,1)S(1)}, u32[]{:S(2)}, u32[]{:S(2)}) collective-permute-start(bf16[2048,256]{0,1:T(8,128)(2,1)S(1)} %pad_maximum_fusion), channel_id=1, source_target_pairs={{0,16},{4,20},{8,24},{12,28},{16,0},{20,4},{24,8},{28,12},{1,17},{... | collective-permute-start | bytes 3145736 | tf_op jit(solution)/shard_map/ppermute | solution.py:78
  49.0 38.4 %copy-start.22 = (s32[4096]{0:T(1024)S(1)}, s32[4096]{0:T(1024)}, u32[]{:S(2)}) copy-start(s32[4096]{0:T(1024)} %param.18) | copy-start | bytes 49156
  49.0 38.4 %copy-start.23 = (s32[1024]{0:T(1024)S(1)}, s32[1024]{0:T(1024)}, u32[]{:S(2)}) copy-start(s32[1024]{0:T(1024)} %param.16) | copy-start | bytes 12292
  87.4 8.2 %copy-start.19 = (bf16[8192,256]{0,1:T(8,128)(2,1)}, bf16[8192,256]{0,1:T(8,128)(2,1)S(1)}, u32[]{:S(2)}) copy-start(bf16[8192,256]{0,1:T(8,128)(2,1)S(1)} %constant_dynamic-update-slice_fusion.2) | copy-start | bytes 12582916
  87.4 8.2 %copy-start.24 = (s32[256]{0:T(256)S(1)}, s32[256]{0:T(256)}, u32[]{:S(2)}) copy-start(s32[256]{0:T(256)} %param.17) | copy-start | bytes 3076
  101.9 11.8 %copy-start.20 = (bf16[8192,256]{0,1:T(8,128)(2,1)S(1)}, bf16[8192,256]{0,1:T(8,128)(2,1)}, u32[]{:S(2)}) copy-start(bf16[8192,256]{0,1:T(8,128)(2,1)} %copy-done.19) | copy-start | bytes 12582916
  110.4 3.2 copy-start.2
  117.1 119.0 %reduce-scatter.5.cloned.1.call-start = ((), (), s32[]{:S(2)}) async-start(), calls=%async_computation.3 | async-start | bytes 4718592 | tf_op jit(solution)/shard_map/reduce_scatter | solution.py:111
  125.0 22.2 %copy-start.9 = (f32[256,1024]{1,0:T(8,128)S(1)}, f32[256,1024]{1,0:T(8,128)}, u32[]{:S(2)}) copy-start(f32[256,1024]{1,0:T(8,128)} %copy-done.8) | copy-start | bytes 3145732
  125.0 22.2 %copy-start.12 = (bf16[256,512]{1,0:T(8,128)(2,1)S(1)}, bf16[256,512]{1,0:T(8,128)(2,1)}, u32[]{:S(2)}) copy-start(bf16[256,512]{1,0:T(8,128)(2,1)} %param.13) | copy-start | bytes 786436
  125.0 316.0 %all-reduce.10.cloned.1.call-start = ((), (), s32[]{:S(2)}) async-start(), calls=%async_computation.4 | async-start | bytes 18874368
  152.6 1.8 copy-start.10
  154.9 1.9 copy-start.6
  156.8 80.6 %copy-start.4 = (bf16[768,512]{1,0:T(8,128)(2,1)S(1)}, bf16[768,512]{1,0:T(8,128)(2,1)}, u32[]{:S(2)}) copy-start(bf16[768,512]{1,0:T(8,128)(2,1)} %copy-done.3) | copy-start | bytes 2359300
  237.1 1.8 copy-start.14
  241.6 1.9 copy-start.17
  249.8 284.9 %copy-start.1 = (bf16[512,1024]{1,0:T(8,128)(2,1)S(1)}, bf16[512,1024]{1,0:T(8,128)(2,1)}, u32[]{:S(2)}) copy-start(bf16[512,1024]{1,0:T(8,128)(2,1)} %param.23) | copy-start | bytes 3145732
  (5 other events, 6.4 us)
Sparse Core Ops, SparseCore 0:
  117.2 26.4 reduce-scatter.2
  147.3 88.6 reduce-scatter.4
  249.9 191.0 all-reduce.9
